TPU v7x, 32 devices: a whole 2x2x4 slice. The times are simulated.
32 devices in a mesh: row: 4 (over y, core), col: 8 (over z, x).
Axes of the slice: x: 2, y: 2, z: 4, core: 2. Of those that a mesh axis runs over, the one named last changes fastest.
Arguments:
- queries: bfloat16 [128, 128, 1024], P(('row', 'col')), may hold values from -6 to 6
- coarse_keys: bfloat16 [512, 1024], P('row'), may hold values from -6 to 6
- fine_keys: bfloat16 [4096, 1024], P('col'), may hold values from -6 to 6
- super_ids: int32 [128, 16], P(('row', 'col')), may hold values from 0 to 511, as said below
- picks: int32 [128, 64], P(('row', 'col')), may hold values from 0 to 127, as said below
Outputs:
- importance: float32 [128, 8, 512], P(('row', 'col'))
- selected: float32 [128, 512], P(('row', 'col'))
Inputs may be any that keep to these rules, and one draw needn't show every extreme that they name: `super_ids`: within each aligned run of 4 query blocks (the query blocks of one device), at most 16 of the ids lie in any one aligned range of 64 superblocks, and some range holds exactly 16; in some aligned group of 8 consecutive runs, one range holds exactly 16 ids of every run. Ids may repeat. `picks`: the numbers of a row are distinct; pick p names fine block p % 8 of superblock super_ids[b, p // 8]. Within each aligned run of 4 query blocks, at most 64 of the named fine blocks lie in any one aligned range of 64 superblocks, and some range holds exactly 64.
All inputs are finite; a program needn't handle non-finite values.
Results may differ from a plain program's by a relative error of at most 0.0003.
Values may be sent and summed in bfloat16 or wider, within the bound.
A program may use at most 64 MiB of HBM per device.

v0:
```python
import math
import jax
import jax.numpy as jnp
from jax import lax
from jax.sharding import PartitionSpec as P

H = 8
D = 128
SBLK = 8
PICK = 64


def pack_requests(owners, local_ids, ncols, capacity):
    marks = (owners[:, None] == jnp.arange(ncols, dtype=jnp.int32)[None, :]).astype(jnp.int32)
    earlier = jnp.cumsum(marks, axis=0) - marks
    slots = jnp.sum(earlier * marks, axis=1)
    places = owners * capacity + slots
    cells = jnp.arange(ncols * capacity, dtype=jnp.int32)
    matches = places[:, None] == cells[None, :]
    outgoing = jnp.sum(jnp.where(matches, local_ids[:, None] + 1, 0), axis=0) - 1
    return (outgoing.reshape(ncols, capacity), places)


def per_device(queries, coarse_keys, fine_keys, super_ids, picks):
    factor = 1.0 / math.sqrt(D)
    blocks, qtok, width = queries.shape
    supers = coarse_keys.shape[0] * lax.axis_size("row")
    ncols = lax.axis_size("col")
    qheads = queries.reshape(blocks, qtok, H, D)

    def block_scores(query_block, block_keys):
        keyed = block_keys.reshape(block_keys.shape[0], H, D)
        return (
            jnp.einsum("thd,nhd->htn", query_block, keyed, preferred_element_type=jnp.float32)
            * factor
        )

    start_max = jnp.full((blocks, H, qtok), -1e30, jnp.float32)
    start_totals = jnp.zeros((blocks, H, qtok), jnp.float32)
    gathered = lax.all_gather(coarse_keys, "row", axis=0, tiled=True)

    def stat_per_block(inputs):
        query_block, running_max, totals = inputs
        scores = block_scores(query_block, gathered)
        new_max = jnp.maximum(running_max, jnp.max(scores, axis=-1))
        totals = totals * jnp.exp(running_max - new_max) + jnp.sum(
            jnp.exp(scores - new_max[..., None]), axis=-1
        )
        return (new_max, totals)

    running_max, totals = lax.map(stat_per_block, (qheads, start_max, start_totals))

    def make_per_block(inputs):
        query_block, block_max, block_totals = inputs
        scores = block_scores(query_block, gathered)
        softened = jnp.exp(scores - block_max[..., None]) / block_totals[..., None]
        return jnp.sum(softened, axis=1) * (supers / qtok)

    portion = lax.map(make_per_block, (qheads, running_max, totals))
    sup_dev = fine_keys.shape[0] // SBLK
    parents = jnp.take_along_axis(super_ids, picks // SBLK, axis=1)
    capacity = blocks // 4 * PICK
    span = sup_dev * SBLK
    fine_ids = parents * SBLK + picks % SBLK
    owners = (fine_ids // span).reshape(-1)
    local_ids = (fine_ids % span).reshape(-1)
    outgoing, places = pack_requests(owners, local_ids, ncols, capacity)
    found = jnp.take(
        fine_keys,
        jnp.clip(
            lax.all_to_all(outgoing, "col", split_axis=0, concat_axis=0, tiled=True), 0, span - 1
        ),
        axis=0,
    )
    replies = lax.all_to_all(found, "col", split_axis=0, concat_axis=0, tiled=True)
    fetched = jnp.take(replies.reshape(ncols * capacity, width), places, axis=0)
    fetched = fetched.reshape(blocks, PICK, H, D)
    weights = jnp.take_along_axis(
        portion, jnp.broadcast_to(parents[:, None, :], (blocks, H, PICK)), axis=2
    )
    scores = (
        jnp.einsum("bthd,bjhd->bhtj", qheads, fetched, preferred_element_type=jnp.float32) * factor
    )
    softened = jax.nn.softmax(scores, axis=-1)
    selected = jnp.sum(softened, axis=2) * weights * (PICK / qtok)
    return (portion, selected.reshape(blocks, H * PICK))


def solution(mesh):
    return jax.shard_map(
        per_device,
        mesh=mesh,
        in_specs=(
            P(("row", "col"), None, None),
            P("row", None),
            P("col", None),
            P(("row", "col"), None),
            P(("row", "col"), None),
        ),
        out_specs=(P(("row", "col"), None, None), P(("row", "col"), None)),
        check_vma=False,
    )
```

profile of v0, /device:TPU:0, one launch (start us, length us, event | category | flops | bytes accessed | tf_op | source)
XLA Modules:
  0.0 85.9 jit_solution(12894194768072370491)
XLA Ops:
  7.2 0.8 bitcast_or_fusion
  8.1 2.3 %gather_fusion.2 = s32[256]{0:T(256)S(1)} fusion(s32[4,16]{1,0:T(4,128)} %param.12, s32[256]{0:T(256)S(1)} %reshape.247), kind=kCustom, calls=%fused_computation.2 | custom fusion | bytes 4096 | tf_op jit(solution)/shard_map/jit(take_along_axis)/gather | solution.py:61
  12.6 7.3 %all-to-all-start = ((s32[8,1,64]{2,1,0:T(1,128)}), s32[8,1,64]{2,1,0:T(1,128)S(1)}, u32[]{:S(2)}, u32[]{:S(2)}) async-start(s32[8,1,64]{2,1,0:T(1,128)} %sub.59), calls=%async_computation | async-start | bytes 8192 | tf_op jit(solution)/shard_map/all_to_all | solution.py:71
  19.9 0.7 all-gather.2.cloned.1.call-update
  21.6 1.0 %copy-done.2 = bf16[4,128,1024]{1,2,0:T(8,128)(2,1)} copy-done((bf16[4,128,1024]{1,2,0:T(8,128)(2,1)}, bf16[4,128,1024]{1,2,0:T(8,128)(2,1)S(1)}, u32[]{:S(2)}) %copy-start.2) | copy-done | bytes 1048600
  23.3 3.0 %all-to-all-done = s32[8,1,64]{2,1,0:T(1,128)S(1)} async-done(((s32[8,1,64]{2,1,0:T(1,128)}), s32[8,1,64]{2,1,0:T(1,128)S(1)}, u32[]{:S(2)}, u32[]{:S(2)}) %all-to-all-start) | async-done | bytes 2080 | tf_op jit(solution)/shard_map/all_to_all | solution.py:71
  26.4 2.1 %gather_fusion = bf16[512,1024]{1,0:T(8,128)(2,1)S(1)} fusion(bf16[512,1024]{1,0:T(8,128)(2,1)S(1)} %copy-done, s32[1024]{0:T(1024)S(1)} %pad_clamp_fusion.1), kind=kCustom, calls=%fused_computation | custom fusion | bytes 2099200 | tf_op jit(solution)/shard_map/jit(_take)/gather | solution.py:68
  28.5 1.2 %broadcast_select_fusion = bf16[8,64,1024]{2,1,0:T(8,128)(2,1)} fusion(bf16[8,64,1024]{2,1,0:T(8,128)(2,1)S(1)} %bitcast.99, pred[8,64]{1,0:T(8,128)(4,1)S(1)} %compare_and_fusion), kind=kLoop, calls=%fused_computation.36 | loop fusion | flops 524288 | bytes 2097664 | tf_op jit(solution)/shard_map/jit(_take)/select_n | solution.py:68
  29.7 3.6 %all-to-all-start.1 = ((bf16[8,64,1024]{2,1,0:T(8,128)(2,1)}), bf16[8,64,1024]{2,1,0:T(8,128)(2,1)S(1)}, u32[]{:S(2)}, u32[]{:S(2)}) async-start(bf16[8,64,1024]{2,1,0:T(8,128)(2,1)} %broadcast_select_fusion), calls=%async_computation.1 | async-start | bytes 2097152 | tf_op jit(solution)/shard_map/all_to_all | solution.py:75
  33.2 7.2 %all-gather.2.cloned.1.call-done = bf16[512,1024]{1,0:T(8,128)(2,1)} async-done(((bf16[128,1024]{1,0:T(8,128)(2,1)}), bf16[512,1024]{1,0:T(8,128)(2,1)}) %all-gather.2.cloned.1.call-update) | async-done | bytes 1048592 | tf_op jit(solution)/shard_map/all_gather | solution.py:40
  40.4 9.6 %while.22 = (s32[]{:T(128)}, f32[4,8,128]{2,1,0:T(8,128)S(1)}, f32[4,8,128]{2,1,0:T(8,128)S(1)}, bf16[4,128,8,128]{3,1,2,0:T(8,128)(2,1)S(1)}, bf16[512,1024]{1,0:T(8,128)(2,1)}, /*index=5*/s32[]{:T(128)}) while((s32[]{:T(128)}, f32[4,8,128]{2,1,0:T(8,128)S(1)}, f32[4,8,128]{2,1,0:T(8,128)S(1)}, bf16[4,128,8,128]{3,1,2,0:T(8,128)(2,1)S(1)}, ...), condition=%wide.region_3.4_spmd, body=%wide.region_0.3_spmd.sunk | while | flops 136842240 | bytes 5541965 | solution.py:51
  40.4 1.8 %multiply_reduce_fusion.2 = (f32[8,128]{1,0:T(8,128)S(1)}, f32[8,128,512]{2,1,0:T(8,128)S(1)}) fusion(bf16[4,128,8,128]{3,1,2,0:T(8,128)(2,1)S(1)} %get-tuple-element.227, s32[]{:T(128)} %get-tuple-element.218, bf16[512,1024]{1,0:T(8,128)(2,1)} %get-tuple-element.228), kind=kOutput, calls=%fused_computation.5.clone.1 | convolution fusion | flops 135265280 | bytes 3411972 | tf_op jit(solution)/shard_map/while/body/eval_jaxpr/thd,nhd->htn/dot_general | solution.py:34
  42.8 1.8 %multiply_reduce_fusion.2 = (f32[8,128]{1,0:T(8,128)S(1)}, f32[8,128,512]{2,1,0:T(8,128)S(1)}) fusion(bf16[4,128,8,128]{3,1,2,0:T(8,128)(2,1)S(1)} %get-tuple-element.227, s32[]{:T(128)} %get-tuple-element.218, bf16[512,1024]{1,0:T(8,128)(2,1)} %get-tuple-element.228), kind=kOutput, calls=%fused_computation.5.clone.1 | convolution fusion | flops 135265280 | bytes 3411972 | tf_op jit(solution)/shard_map/while/body/eval_jaxpr/thd,nhd->htn/dot_general | solution.py:34
  45.2 1.8 %multiply_reduce_fusion.2 = (f32[8,128]{1,0:T(8,128)S(1)}, f32[8,128,512]{2,1,0:T(8,128)S(1)}) fusion(bf16[4,128,8,128]{3,1,2,0:T(8,128)(2,1)S(1)} %get-tuple-element.227, s32[]{:T(128)} %get-tuple-element.218, bf16[512,1024]{1,0:T(8,128)(2,1)} %get-tuple-element.228), kind=kOutput, calls=%fused_computation.5.clone.1 | convolution fusion | flops 135265280 | bytes 3411972 | tf_op jit(solution)/shard_map/while/body/eval_jaxpr/thd,nhd->htn/dot_general | solution.py:34
  47.6 1.8 %multiply_reduce_fusion.2 = (f32[8,128]{1,0:T(8,128)S(1)}, f32[8,128,512]{2,1,0:T(8,128)S(1)}) fusion(bf16[4,128,8,128]{3,1,2,0:T(8,128)(2,1)S(1)} %get-tuple-element.227, s32[]{:T(128)} %get-tuple-element.218, bf16[512,1024]{1,0:T(8,128)(2,1)} %get-tuple-element.228), kind=kOutput, calls=%fused_computation.5.clone.1 | convolution fusion | flops 135265280 | bytes 3411972 | tf_op jit(solution)/shard_map/while/body/eval_jaxpr/thd,nhd->htn/dot_general | solution.py:34
  50.0 8.1 %while.23 = (s32[]{:T(128)}, f32[4,8,512]{2,1,0:T(8,128)S(1)}, bf16[4,128,8,128]{3,1,2,0:T(8,128)(2,1)S(1)}, bf16[512,1024]{1,0:T(8,128)(2,1)}, f32[4,8,128]{2,1...) while((s32[]{:T(128)}, f32[4,8,512]{2,1,0:T(8,128)S(1)}, bf16[4,128,8,128]{3,1,2,0:T(8,128)(2,1)S(1)}, ...), condition=%wide.region_6.7_spmd, body=%wide.region_4.6_spmd.sunk | while | flops 136314880 | bytes 1384537 | solution.py:59
  50.0 2.0 %fusion.49 = f32[8,512]{1,0:T(8,128)S(1)} fusion(f32[8,128]{1,0:T(8,128)S(1)} %get-tuple-element.210, f32[8,128]{1,0:T(8,128)S(1)} %get-tuple-element.211, bf16[4,128,8,128]{3,1,2,0:T(8,128)(2,1)S(1)} %get-tuple-element.246, s32[]{:T(128)} %get-tuple-element.237, bf16[512,1024]{1,0:T(8,128)(2,1)} %get-tuple-element.247), kind=kOutput, calls=%fused_computation.20.clone.1 | convolution fusion | flops 136310784 | bytes 1335300 | tf_op jit(solution)/shard_map/while/body/eval_jaxpr/thd,nhd->htn/dot_general | solution.py:34
  52.1 2.0 %fusion.49 = f32[8,512]{1,0:T(8,128)S(1)} fusion(f32[8,128]{1,0:T(8,128)S(1)} %get-tuple-element.210, f32[8,128]{1,0:T(8,128)S(1)} %get-tuple-element.211, bf16[4,128,8,128]{3,1,2,0:T(8,128)(2,1)S(1)} %get-tuple-element.246, s32[]{:T(128)} %get-tuple-element.237, bf16[512,1024]{1,0:T(8,128)(2,1)} %get-tuple-element.247), kind=kOutput, calls=%fused_computation.20.clone.1 | convolution fusion | flops 136310784 | bytes 1335300 | tf_op jit(solution)/shard_map/while/body/eval_jaxpr/thd,nhd->htn/dot_general | solution.py:34
  54.1 2.0 %fusion.49 = f32[8,512]{1,0:T(8,128)S(1)} fusion(f32[8,128]{1,0:T(8,128)S(1)} %get-tuple-element.210, f32[8,128]{1,0:T(8,128)S(1)} %get-tuple-element.211, bf16[4,128,8,128]{3,1,2,0:T(8,128)(2,1)S(1)} %get-tuple-element.246, s32[]{:T(128)} %get-tuple-element.237, bf16[512,1024]{1,0:T(8,128)(2,1)} %get-tuple-element.247), kind=kOutput, calls=%fused_computation.20.clone.1 | convolution fusion | flops 136310784 | bytes 1335300 | tf_op jit(solution)/shard_map/while/body/eval_jaxpr/thd,nhd->htn/dot_general | solution.py:34
  56.1 2.0 %fusion.49 = f32[8,512]{1,0:T(8,128)S(1)} fusion(f32[8,128]{1,0:T(8,128)S(1)} %get-tuple-element.210, f32[8,128]{1,0:T(8,128)S(1)} %get-tuple-element.211, bf16[4,128,8,128]{3,1,2,0:T(8,128)(2,1)S(1)} %get-tuple-element.246, s32[]{:T(128)} %get-tuple-element.237, bf16[512,1024]{1,0:T(8,128)(2,1)} %get-tuple-element.247), kind=kOutput, calls=%fused_computation.20.clone.1 | convolution fusion | flops 136310784 | bytes 1335300 | tf_op jit(solution)/shard_map/while/body/eval_jaxpr/thd,nhd->htn/dot_general | solution.py:34
  58.1 16.3 %gather_fusion.3 = f32[2048]{0:T(1024)S(1)} fusion(f32[4,8,512]{2,1,0:T(8,128)S(1)} %get-tuple-element.60, s32[2048]{0:T(1024)S(1)} %reshape.253), kind=kCustom, calls=%fused_computation.3 | custom fusion | bytes 40960 | tf_op jit(solution)/shard_map/jit(take_along_axis)/gather | solution.py:78
  74.5 2.0 %gather_fusion.1 = bf16[256,1024]{1,0:T(8,128)(2,1)} fusion(bf16[512,1024]{1,0:T(8,128)(2,1)S(1)} %bitcast.98, s32[1024]{0:T(1024)S(1)} %pad_clamp_fusion), kind=kCustom, calls=%fused_computation.1 | custom fusion | bytes 1049600 | tf_op jit(solution)/shard_map/jit(_take)/gather | solution.py:76
  76.5 1.1 %copy.34 = bf16[32,8,8,128]{3,2,1,0:T(8,128)(2,1)S(1)} copy(bf16[32,8,8,128]{3,1,2,0:T(8,128)(2,1)} %bitcast.102) | data formatting | bytes 1048576
  77.6 0.7 fusion.34
  (71 shorter events, 7.2 us)
Async XLA Ops:
  7.2 19.3 %copy-start = (bf16[512,1024]{1,0:T(8,128)(2,1)S(1)}, bf16[512,1024]{1,0:T(8,128)(2,1)}, u32[]{:S(2)}) copy-start(bf16[512,1024]{1,0:T(8,128)(2,1)} %param.11) | copy-start | bytes 3145732
  7.2 3.4 %copy-start.5 = (s32[4,64]{1,0:T(4,128)S(1)}, s32[4,64]{1,0:T(4,128)}, u32[]{:S(2)}) copy-start(s32[4,64]{1,0:T(4,128)} %param.13) | copy-start | bytes 3076
  7.2 13.7 %copy-start.4 = (bf16[4,128,1024]{2,1,0:T(8,128)(2,1)S(1)}, bf16[4,128,1024]{2,1,0:T(8,128)(2,1)}, u32[]{:S(2)}) copy-start(bf16[4,128,1024]{2,1,0:T(8,128)(2,1)} %param.9) | copy-start | bytes 3145732
  12.6 13.7 %all-to-all-start = ((s32[8,1,64]{2,1,0:T(1,128)}), s32[8,1,64]{2,1,0:T(1,128)S(1)}, u32[]{:S(2)}, u32[]{:S(2)}) async-start(s32[8,1,64]{2,1,0:T(1,128)} %sub.59), calls=%async_computation | async-start | bytes 8192 | tf_op jit(solution)/shard_map/all_to_all | solution.py:71
  19.9 20.5 %all-gather.2.cloned.1.call-start = ((), (), s32[]{:S(2)}) async-start(), calls=%async_computation.2 | async-start | bytes 1310720 | tf_op jit(solution)/shard_map/all_gather | solution.py:40
  21.6 1.0 %copy-start.2 = (bf16[4,128,1024]{1,2,0:T(8,128)(2,1)}, bf16[4,128,1024]{1,2,0:T(8,128)(2,1)S(1)}, u32[]{:S(2)}) copy-start(bf16[4,128,1024]{1,2,0:T(8,128)(2,1)S(1)} %copy.26) | copy-start | bytes 3145732
  29.7 44.8 %all-to-all-start.1 = ((bf16[8,64,1024]{2,1,0:T(8,128)(2,1)}), bf16[8,64,1024]{2,1,0:T(8,128)(2,1)S(1)}, u32[]{:S(2)}, u32[]{:S(2)}) async-start(bf16[8,64,1024]{2,1,0:T(8,128)(2,1)} %broadcast_select_fusion), calls=%async_computation.1 | async-start | bytes 2097152 | tf_op jit(solution)/shard_map/all_to_all | solution.py:75
  58.1 16.3 %copy-start.1 = (f32[4,8,512]{2,1,0:T(8,128)}, f32[4,8,512]{2,1,0:T(8,128)S(1)}, u32[]{:S(2)}) copy-start(f32[4,8,512]{2,1,0:T(8,128)S(1)} %get-tuple-element.60) | copy-start | bytes 196612
  74.5 3.1 %copy-start.3 = (bf16[4,128,1024]{1,2,0:T(8,128)(2,1)S(1)}, bf16[4,128,1024]{1,2,0:T(8,128)(2,1)}, u32[]{:S(2)}) copy-start(bf16[4,128,1024]{1,2,0:T(8,128)(2,1)} %copy-done.2) | copy-start | bytes 3145732
Sparse Core Ops, SparseCore 0:
  22.3 18.1 all-gather.1
where the time goes:
time: 86.5 us; the launch traced here: 85.9 us
  local copies, waits for them, and re-layouts  28.5 us (33%)
  matrix products  15.6 us (18%)
  between operations  14.3 us (17%)
  starting transfers between devices  10.9 us (13%)
  waiting for transfers between devices  10.9 us (13%)
  other arithmetic  5.45 us (6%)
    gather x3, local copies, waits for them, and re-layouts, per_device(): jnp.take_along_axis(portion, jnp.broadcast_to(parents[:, None, :], (block...  16.4 us
    dot_general x8, matrix products, block_scores(): jnp.einsum('thd,nhd->htn', query_block, keyed, preferred_element_type=jnp...  14.9 us
    all_to_all x1, starting transfers between devices, per_device(): lax.all_to_all(outgoing, 'col', split_axis=0, concat_axis=0, tiled=True)  7.28 us
    all_gather x1, waiting for transfers between devices, per_device(): gathered = lax.all_gather(coarse_keys, 'row', axis=0, tiled=True)  7.22 us
    all_to_all x1, starting transfers between devices, per_device(): lax.all_to_all(found, 'col', split_axis=0, concat_axis=0, tiled=True)  3.56 us
    all_to_all x1, waiting for transfers between devices, per_device(): lax.all_to_all(outgoing, 'col', split_axis=0, concat_axis=0, tiled=True)  3.04 us
    unnamed x14, local copies, waits for them, and re-layouts  2.8 us
    gather x3, local copies, waits for them, and re-layouts, per_device(): parents = jnp.take_along_axis(super_ids, picks // SBLK, axis=1)  2.49 us
  transfers between devices with their start and end apart: 3, of which 2 were waited for; matrix products, arithmetic and copies ran while one was open for 45% of the time, Pallas kernels for 0%

commit v1 on v0

--- a/solution.py
+++ b/solution.py
@@ -8,6 +8,17 @@
 D = 128
 SBLK = 8
 PICK = 64
+
+
+def pass_along(array, name, dim):
+    size = lax.axis_size(name)
+    route = [(i, (i + 1) % size) for i in range(size)]
+    parts = [array]
+    for hop in range(1, size):
+        parts = [lax.ppermute(parts[0], name, route), *parts]
+    out = jnp.concatenate(parts, axis=dim)
+    shift = (lax.axis_index(name) + 1) * parts[-1].shape[dim]
+    return jnp.roll(out, shift, axis=dim)
 
 
 def pack_requests(owners, local_ids, ncols, capacity):
@@ -37,7 +48,7 @@
 
     start_max = jnp.full((blocks, H, qtok), -1e30, jnp.float32)
     start_totals = jnp.zeros((blocks, H, qtok), jnp.float32)
-    gathered = lax.all_gather(coarse_keys, "row", axis=0, tiled=True)
+    gathered = pass_along(coarse_keys, "row", 0)
 
     def stat_per_block(inputs):
         query_block, running_max, totals = inputs

time: 86.5 us -> 69.1 us (0.80)
  between operations: 14.3 us -> 0.96 us
  waiting for transfers between devices: 10.9 us -> 7.64 us
  matrix products: 15.6 us -> 13.4 us
  local copies, waits for them, and re-layouts: 28.5 us -> 29.4 us
    all_gather x1 -> x0, waiting for transfers between devices: 7.22 us -> none  [per_device(): gathered = lax.all_gather(coarse_keys, 'row', axis=0, tiled=True)]
    ppermute x0 -> x3, waiting for transfers between devices: none -> 4.55 us  [pass_along(): parts = [lax.ppermute(parts[0], name, route), *parts]]
    dot_general x8, matrix products: 14.9 us -> 12.7 us  [block_scores(): jnp.einsum('thd,nhd->htn', query_block, keyed, preferred_element_type=jnp...]
    unnamed x14 -> x23, local copies, waits for them, and re-layouts: 2.8 us -> 2.94 us
  transfers between devices with their start and end apart: 3 -> 5, of which waited for: 2 -> 3; matrix products, arithmetic and copies ran while one was open for 45% -> 62% of each run, Pallas kernels for 0% -> 0%
where the time goes in v1:
time: 69.1 us; the launch traced here: 68.3 us
  local copies, waits for them, and re-layouts  29.4 us (43%)
  matrix products  13.4 us (19%)
  starting transfers between devices  11.2 us (16%)
  waiting for transfers between devices  7.64 us (11%)
  other arithmetic  5.35 us (8%)
  between operations  0.96 us (1%)
    gather x3, local copies, waits for them, and re-layouts, per_device(): jnp.take_along_axis(portion, jnp.broadcast_to(parents[:, None, :], (block...  16.4 us
    dot_general x8, matrix products, block_scores(): jnp.einsum('thd,nhd->htn', query_block, keyed, preferred_element_type=jnp...  12.7 us
    all_to_all x1, starting transfers between devices, per_device(): lax.all_to_all(outgoing, 'col', split_axis=0, concat_axis=0, tiled=True)  6.94 us
    ppermute x3, waiting for transfers between devices, pass_along(): parts = [lax.ppermute(parts[0], name, route), *parts]  4.55 us
    all_to_all x1, starting transfers between devices, per_device(): lax.all_to_all(found, 'col', split_axis=0, concat_axis=0, tiled=True)  3.69 us
    all_to_all x1, waiting for transfers between devices, per_device(): lax.all_to_all(outgoing, 'col', split_axis=0, concat_axis=0, tiled=True)  3.09 us
    unnamed x23, local copies, waits for them, and re-layouts  2.94 us
    gather x3, local copies, waits for them, and re-layouts, per_device(): parents = jnp.take_along_axis(super_ids, picks // SBLK, axis=1)  2.49 us
  transfers between devices with their start and end apart: 5, of which 3 were waited for; matrix products, arithmetic and copies ran while one was open for 62% of the time, Pallas kernels for 0%

profile of v1, /device:TPU:0, one launch (start us, length us, event | category | flops | bytes accessed | tf_op | source)
XLA Modules:
  0.0 68.3 jit_solution(7427949627741404073)
XLA Ops:
  2.0 2.3 %gather_fusion.2 = s32[256]{0:T(256)S(1)} fusion(s32[4,16]{1,0:T(4,128)} %param.12, s32[256]{0:T(256)S(1)} %reshape.247), kind=kCustom, calls=%fused_computation.2 | custom fusion | bytes 4096 | tf_op jit(solution)/shard_map/jit(take_along_axis)/gather | solution.py:72
  6.5 6.9 %all-to-all-start = ((s32[8,1,64]{2,1,0:T(1,128)}), s32[8,1,64]{2,1,0:T(1,128)S(1)}, u32[]{:S(2)}, u32[]{:S(2)}) async-start(s32[8,1,64]{2,1,0:T(1,128)} %sub.64), calls=%async_computation | async-start | bytes 8192 | tf_op jit(solution)/shard_map/all_to_all | solution.py:82
  14.4 1.0 %copy-done.2 = bf16[4,128,1024]{1,2,0:T(8,128)(2,1)} copy-done((bf16[4,128,1024]{1,2,0:T(8,128)(2,1)}, bf16[4,128,1024]{1,2,0:T(8,128)(2,1)S(1)}, u32[]{:S(2)}) %copy-start.2) | copy-done | bytes 1048600
  15.4 1.3 %copy.28 = bf16[4,128,8,128]{3,1,2,0:T(8,128)(2,1)} copy(bf16[4,128,8,128]{1,3,2,0:T(8,128)(2,1)S(1)} %bitcast.100) | data formatting | bytes 2097152 | tf_op jit(solution)/shard_map/while | solution.py:70
  16.8 3.1 %all-to-all-done = s32[8,1,64]{2,1,0:T(1,128)S(1)} async-done(((s32[8,1,64]{2,1,0:T(1,128)}), s32[8,1,64]{2,1,0:T(1,128)S(1)}, u32[]{:S(2)}, u32[]{:S(2)}) %all-to-all-start) | async-done | bytes 2080 | tf_op jit(solution)/shard_map/all_to_all | solution.py:82
  20.0 2.1 %gather_fusion = bf16[512,1024]{1,0:T(8,128)(2,1)S(1)} fusion(bf16[512,1024]{1,0:T(8,128)(2,1)S(1)} %copy-done, s32[1024]{0:T(1024)S(1)} %pad_clamp_fusion.1), kind=kCustom, calls=%fused_computation | custom fusion | bytes 2099200 | tf_op jit(solution)/shard_map/jit(_take)/gather | solution.py:79
  22.1 3.6 %collective-permute-done.1 = bf16[128,1024]{1,0:T(8,128)(2,1)S(1)} collective-permute-done((bf16[128,1024]{1,0:T(8,128)(2,1)S(1)}, bf16[128,1024]{1,0:T(8,128)(2,1)S(1)}, u32[]{:S(2)}, u32[]{:S(2)}) %collective-permute-start.1) | collective-permute-done | bytes 262176 | tf_op jit(solution)/shard_map/ppermute | solution.py:18
  25.7 1.2 %broadcast_select_fusion = bf16[8,64,1024]{2,1,0:T(8,128)(2,1)} fusion(bf16[8,64,1024]{2,1,0:T(8,128)(2,1)S(1)} %bitcast.99, pred[8,64]{1,0:T(8,128)(4,1)S(1)} %compare_and_fusion), kind=kLoop, calls=%fused_computation.36 | loop fusion | flops 524288 | bytes 2097664 | tf_op jit(solution)/shard_map/jit(_take)/select_n | solution.py:79
  26.9 3.7 %all-to-all-start.1 = ((bf16[8,64,1024]{2,1,0:T(8,128)(2,1)}), bf16[8,64,1024]{2,1,0:T(8,128)(2,1)S(1)}, u32[]{:S(2)}, u32[]{:S(2)}) async-start(bf16[8,64,1024]{2,1,0:T(8,128)(2,1)} %broadcast_select_fusion), calls=%async_computation.1 | async-start | bytes 2097152 | tf_op jit(solution)/shard_map/all_to_all | solution.py:86
  30.6 0.9 %collective-permute-done.2 = bf16[128,1024]{1,0:T(8,128)(2,1)S(1)} collective-permute-done((bf16[128,1024]{1,0:T(8,128)(2,1)S(1)}, bf16[128,1024]{1,0:T(8,128)(2,1)S(1)}, u32[]{:S(2)}, u32[]{:S(2)}) %collective-permute-start.2) | collective-permute-done | bytes 262176 | tf_op jit(solution)/shard_map/ppermute | solution.py:18
  31.8 8.5 %while.22 = (s32[]{:T(128)}, f32[4,8,128]{2,1,0:T(8,128)S(1)}, f32[4,8,128]{2,1,0:T(8,128)S(1)}, bf16[4,128,8,128]{3,1,2,0:T(8,128)(2,1)}, bf16[512,1024]{1,0:T(8,128)(2,1)S(1)}, /*index=5*/s32[]{:T(128)}) while((s32[]{:T(128)}, f32[4,8,128]{2,1,0:T(8,128)S(1)}, f32[4,8,128]{2,1,0:T(8,128)S(1)}, bf16[4,128,8,128]{3,1,2,0:T(8,128)(2,1)}, ...), condition=%wide.region_3.4_spmd, body=%wide.region_0.3_spmd.sunk | while | flops 136842240 | bytes 5542473 | solution.py:62
  31.9 1.5 %multiply_reduce_fusion.2 = (f32[8,128]{1,0:T(8,128)S(1)}, f32[8,128,512]{2,1,0:T(8,128)S(1)}) fusion(bf16[4,128,8,128]{3,1,2,0:T(8,128)(2,1)} %get-tuple-element.227, s32[]{:T(128)} %get-tuple-element.218, bf16[512,1024]{1,0:T(8,128)(2,1)S(1)} %get-tuple-element.228), kind=kOutput, calls=%fused_computation.5.clone.1 | convolution fusion | flops 135265280 | bytes 3412480 | tf_op jit(solution)/shard_map/while/body/eval_jaxpr/thd,nhd->htn/dot_general | solution.py:45
  34.0 1.5 %multiply_reduce_fusion.2 = (f32[8,128]{1,0:T(8,128)S(1)}, f32[8,128,512]{2,1,0:T(8,128)S(1)}) fusion(bf16[4,128,8,128]{3,1,2,0:T(8,128)(2,1)} %get-tuple-element.227, s32[]{:T(128)} %get-tuple-element.218, bf16[512,1024]{1,0:T(8,128)(2,1)S(1)} %get-tuple-element.228), kind=kOutput, calls=%fused_computation.5.clone.1 | convolution fusion | flops 135265280 | bytes 3412480 | tf_op jit(solution)/shard_map/while/body/eval_jaxpr/thd,nhd->htn/dot_general | solution.py:45
  36.1 1.5 %multiply_reduce_fusion.2 = (f32[8,128]{1,0:T(8,128)S(1)}, f32[8,128,512]{2,1,0:T(8,128)S(1)}) fusion(bf16[4,128,8,128]{3,1,2,0:T(8,128)(2,1)} %get-tuple-element.227, s32[]{:T(128)} %get-tuple-element.218, bf16[512,1024]{1,0:T(8,128)(2,1)S(1)} %get-tuple-element.228), kind=kOutput, calls=%fused_computation.5.clone.1 | convolution fusion | flops 135265280 | bytes 3412480 | tf_op jit(solution)/shard_map/while/body/eval_jaxpr/thd,nhd->htn/dot_general | solution.py:45
  38.2 1.5 %multiply_reduce_fusion.2 = (f32[8,128]{1,0:T(8,128)S(1)}, f32[8,128,512]{2,1,0:T(8,128)S(1)}) fusion(bf16[4,128,8,128]{3,1,2,0:T(8,128)(2,1)} %get-tuple-element.227, s32[]{:T(128)} %get-tuple-element.218, bf16[512,1024]{1,0:T(8,128)(2,1)S(1)} %get-tuple-element.228), kind=kOutput, calls=%fused_computation.5.clone.1 | convolution fusion | flops 135265280 | bytes 3412480 | tf_op jit(solution)/shard_map/while/body/eval_jaxpr/thd,nhd->htn/dot_general | solution.py:45
  40.3 7.0 %while.23 = (s32[]{:T(128)}, f32[4,8,512]{2,1,0:T(8,128)S(1)}, bf16[4,128,8,128]{3,1,2,0:T(8,128)(2,1)}, bf16[512,1024]{1,0:T(8,128)(2,1)S(1)}, f32[4,8,128]{2,1...) while((s32[]{:T(128)}, f32[4,8,512]{2,1,0:T(8,128)S(1)}, bf16[4,128,8,128]{3,1,2,0:T(8,128)(2,1)}, ...), condition=%wide.region_6.7_spmd, body=%wide.region_4.6_spmd.sunk | while | flops 136314880 | bytes 1385045 | solution.py:70
  40.4 1.7 %fusion.49 = f32[8,512]{1,0:T(8,128)S(1)} fusion(f32[8,128]{1,0:T(8,128)S(1)} %get-tuple-element.210, f32[8,128]{1,0:T(8,128)S(1)} %get-tuple-element.211, bf16[4,128,8,128]{3,1,2,0:T(8,128)(2,1)} %get-tuple-element.246, s32[]{:T(128)} %get-tuple-element.237, bf16[512,1024]{1,0:T(8,128)(2,1)S(1)} %get-tuple-element.247), kind=kOutput, calls=%fused_computation.20.clone.1 | convolution fusion | flops 136310784 | bytes 1335808 | tf_op jit(solution)/shard_map/while/body/eval_jaxpr/thd,nhd->htn/dot_general | solution.py:45
  42.1 1.7 %fusion.49 = f32[8,512]{1,0:T(8,128)S(1)} fusion(f32[8,128]{1,0:T(8,128)S(1)} %get-tuple-element.210, f32[8,128]{1,0:T(8,128)S(1)} %get-tuple-element.211, bf16[4,128,8,128]{3,1,2,0:T(8,128)(2,1)} %get-tuple-element.246, s32[]{:T(128)} %get-tuple-element.237, bf16[512,1024]{1,0:T(8,128)(2,1)S(1)} %get-tuple-element.247), kind=kOutput, calls=%fused_computation.20.clone.1 | convolution fusion | flops 136310784 | bytes 1335808 | tf_op jit(solution)/shard_map/while/body/eval_jaxpr/thd,nhd->htn/dot_general | solution.py:45
  43.9 1.7 %fusion.49 = f32[8,512]{1,0:T(8,128)S(1)} fusion(f32[8,128]{1,0:T(8,128)S(1)} %get-tuple-element.210, f32[8,128]{1,0:T(8,128)S(1)} %get-tuple-element.211, bf16[4,128,8,128]{3,1,2,0:T(8,128)(2,1)} %get-tuple-element.246, s32[]{:T(128)} %get-tuple-element.237, bf16[512,1024]{1,0:T(8,128)(2,1)S(1)} %get-tuple-element.247), kind=kOutput, calls=%fused_computation.20.clone.1 | convolution fusion | flops 136310784 | bytes 1335808 | tf_op jit(solution)/shard_map/while/body/eval_jaxpr/thd,nhd->htn/dot_general | solution.py:45
  45.6 1.7 %fusion.49 = f32[8,512]{1,0:T(8,128)S(1)} fusion(f32[8,128]{1,0:T(8,128)S(1)} %get-tuple-element.210, f32[8,128]{1,0:T(8,128)S(1)} %get-tuple-element.211, bf16[4,128,8,128]{3,1,2,0:T(8,128)(2,1)} %get-tuple-element.246, s32[]{:T(128)} %get-tuple-element.237, bf16[512,1024]{1,0:T(8,128)(2,1)S(1)} %get-tuple-element.247), kind=kOutput, calls=%fused_computation.20.clone.1 | convolution fusion | flops 136310784 | bytes 1335808 | tf_op jit(solution)/shard_map/while/body/eval_jaxpr/thd,nhd->htn/dot_general | solution.py:45
  47.4 16.3 %gather_fusion.3 = f32[2048]{0:T(1024)S(1)} fusion(f32[4,8,512]{2,1,0:T(8,128)S(1)} %get-tuple-element.60, s32[2048]{0:T(1024)S(1)} %reshape.253), kind=kCustom, calls=%fused_computation.3 | custom fusion | bytes 40960 | tf_op jit(solution)/shard_map/jit(take_along_axis)/gather | solution.py:89
  63.7 2.0 %gather_fusion.1 = bf16[256,1024]{1,0:T(8,128)(2,1)} fusion(bf16[512,1024]{1,0:T(8,128)(2,1)S(1)} %bitcast.98, s32[1024]{0:T(1024)S(1)} %pad_clamp_fusion), kind=kCustom, calls=%fused_computation.1 | custom fusion | bytes 1049600 | tf_op jit(solution)/shard_map/jit(_take)/gather | solution.py:87
  65.7 1.1 %copy.34 = bf16[32,8,8,128]{3,2,1,0:T(8,128)(2,1)S(1)} copy(bf16[32,8,8,128]{3,1,2,0:T(8,128)(2,1)} %bitcast.102) | data formatting | bytes 1048576
  66.8 0.7 %fusion.34 = f32[4,8,64]{2,1,0:T(8,128)S(1)} fusion(bf16[4,128,8,128]{1,3,2,0:T(8,128)(2,1)S(1)} %bitcast.101, bf16[4,64,8,128]{3,2,1,0:T(8,128)(2,1)S(1)} %bitcast.103, pred[4,64]{1,0:T(4,128)(4,1)S(1)} %compare_and_fusion.1), kind=kOutput, calls=%fused_computation.100 | convolution fusion | flops 68425856 | bytes 1581312 | tf_op jit(solution)/shard_map/div | solution.py:95
  (85 shorter events, 8.1 us)
Async XLA Ops:
  0.6 19.4 %copy-start = (bf16[512,1024]{1,0:T(8,128)(2,1)S(1)}, bf16[512,1024]{1,0:T(8,128)(2,1)}, u32[]{:S(2)}) copy-start(bf16[512,1024]{1,0:T(8,128)(2,1)} %param.11) | copy-start | bytes 3145732
  0.6 3.8 %copy-start.6 = (s32[4,64]{1,0:T(4,128)S(1)}, s32[4,64]{1,0:T(4,128)}, u32[]{:S(2)}) copy-start(s32[4,64]{1,0:T(4,128)} %param.13) | copy-start | bytes 3076
  0.7 13.0 %copy-start.4 = (bf16[4,128,1024]{2,1,0:T(8,128)(2,1)S(1)}, bf16[4,128,1024]{2,1,0:T(8,128)(2,1)}, u32[]{:S(2)}) copy-start(bf16[4,128,1024]{2,1,0:T(8,128)(2,1)} %param.9) | copy-start | bytes 3145732
  0.7 19.3 %collective-permute-start = (bf16[128,1024]{1,0:T(8,128)(2,1)}, bf16[128,1024]{1,0:T(8,128)(2,1)S(1)}, u32[]{:S(2)}, u32[]{:S(2)}) collective-permute-start(bf16[128,1024]{1,0:T(8,128)(2,1)} %param.10), channel_id=1, source_target_pairs={{0,8},{8,16},{16,24},{24,0},{1,9},{9,17},{17,25},{25,1},{2,10},{10... | collective-permute-start | bytes 786440 | tf_op jit(solution)/shard_map/ppermute | solution.py:18
  6.5 13.4 %all-to-all-start = ((s32[8,1,64]{2,1,0:T(1,128)}), s32[8,1,64]{2,1,0:T(1,128)S(1)}, u32[]{:S(2)}, u32[]{:S(2)}) async-start(s32[8,1,64]{2,1,0:T(1,128)} %sub.64), calls=%async_computation | async-start | bytes 8192 | tf_op jit(solution)/shard_map/all_to_all | solution.py:82
  14.4 1.0 %copy-start.2 = (bf16[4,128,1024]{1,2,0:T(8,128)(2,1)}, bf16[4,128,1024]{1,2,0:T(8,128)(2,1)S(1)}, u32[]{:S(2)}) copy-start(bf16[4,128,1024]{1,2,0:T(8,128)(2,1)S(1)} %copy.26) | copy-start | bytes 3145732
  19.9 5.8 %collective-permute-start.1 = (bf16[128,1024]{1,0:T(8,128)(2,1)S(1)}, bf16[128,1024]{1,0:T(8,128)(2,1)S(1)}, u32[]{:S(2)}, u32[]{:S(2)}) collective-permute-start(bf16[128,1024]{1,0:T(8,128)(2,1)S(1)} %collective-permute-done), channel_id=1, source_target_pairs={{0,8},{8,16},{16,24},{24,0},{1,9},{9,17},{17,25},{25,1},{2,10},{10... | collective-permute-start | bytes 786440 | tf_op jit(solution)/shard_map/ppermute | solution.py:18
  25.7 5.8 %collective-permute-start.2 = (bf16[128,1024]{1,0:T(8,128)(2,1)S(1)}, bf16[128,1024]{1,0:T(8,128)(2,1)S(1)}, u32[]{:S(2)}, u32[]{:S(2)}) collective-permute-start(bf16[128,1024]{1,0:T(8,128)(2,1)S(1)} %collective-permute-done.1), channel_id=1, source_target_pairs={{0,8},{8,16},{16,24},{24,0},{1,9},{9,17},{17,25},{25,1},{2,10},{10... | collective-permute-start | bytes 786440 | tf_op jit(solution)/shard_map/ppermute | solution.py:18
  26.9 4.7 %copy-start.5 = (bf16[128,1024]{1,0:T(8,128)(2,1)S(1)}, bf16[128,1024]{1,0:T(8,128)(2,1)}, u32[]{:S(2)}) copy-start(bf16[128,1024]{1,0:T(8,128)(2,1)} %param.10) | copy-start | bytes 786436
  26.9 36.8 %all-to-all-start.1 = ((bf16[8,64,1024]{2,1,0:T(8,128)(2,1)}), bf16[8,64,1024]{2,1,0:T(8,128)(2,1)S(1)}, u32[]{:S(2)}, u32[]{:S(2)}) async-start(bf16[8,64,1024]{2,1,0:T(8,128)(2,1)} %broadcast_select_fusion), calls=%async_computation.1 | async-start | bytes 2097152 | tf_op jit(solution)/shard_map/all_to_all | solution.py:86
  47.3 16.3 %copy-start.1 = (f32[4,8,512]{2,1,0:T(8,128)}, f32[4,8,512]{2,1,0:T(8,128)S(1)}, u32[]{:S(2)}) copy-start(f32[4,8,512]{2,1,0:T(8,128)S(1)} %get-tuple-element.60) | copy-start | bytes 196612
  63.7 3.1 %copy-start.3 = (bf16[4,128,1024]{1,2,0:T(8,128)(2,1)S(1)}, bf16[4,128,1024]{1,2,0:T(8,128)(2,1)}, u32[]{:S(2)}) copy-start(bf16[4,128,1024]{1,2,0:T(8,128)(2,1)} %copy-done.2) | copy-start | bytes 3145732
